TPU v7x, 32 devices: a whole 2x2x4 slice. The times are simulated.
32 devices in a mesh: band: 32 (over z, y, x, core).
Axes of the slice: x: 2, y: 2, z: 4, core: 2. Of those that a mesh axis runs over, the one named last changes fastest.
Arguments:
- jones_start: float32 [32, 32, 512], P('band'), may hold values from -1.5 to 1.5
- visible: bfloat16 [32, 8, 4096], P('band'), may hold values from -6 to 6
- coherent: bfloat16 [32, 32, 4096], P('band'), may hold values from -1 to 1
- stations: int32 [2, 4096], replicated, may hold values from 0 to 511, as said below
- weights: float32 [32, 512], P('band'), may hold values from 0.2 to 2
- multiplier_start: float32 [32, 32, 512], P('band'), may hold values from -2 to 2
Outputs:
- jones_final: float32 [32, 32, 512], P('band')
- multiplier_final: float32 [32, 32, 512], P('band')
- coefficients: float32 [96, 512], P(None, 'band')
Inputs may be any that keep to these rules, and one draw needn't show every extreme that they name: Rows 0 and 1 of each column name two different stations; the same baselines serve every subband.
All inputs are finite; a program needn't handle non-finite values.
Results may differ from a plain program's by a relative error of at most 0.0003.
Values sent between devices are 32-bit elements; how exact they have to be, the bound alone decides.
A program may use at most 64 MiB of HBM per device.

v0:
```python
import jax
import jax.numpy as jnp
from jax import lax
from jax.sharding import PartitionSpec as P

ITERS = 2


PENALTY = 1.0
STEP_SIZE = 0.05
PAIR_LIST = ((0, 0), (0, 1), (0, 2), (1, 1), (1, 2), (2, 2))


def matrix_product(first_real, first_imag, second_real, second_imag):

    def contract(lhs_part, rhs_part):
        return jnp.sum(lhs_part[:, :, :, None, :] * rhs_part[:, None, :, :, :], axis=2)

    real_part = contract(first_real, second_real) - contract(first_imag, second_imag)
    imag_part = contract(first_real, second_imag) + contract(first_imag, second_real)
    return (real_part, imag_part)


def band_loss(
    jones_band, visible_band, coherent_band, stations, target_band, multiplier_band, weight_band
):
    baseline_count = stations.shape[1]
    direction_count = jones_band.shape[0] // 8
    station_first = jnp.take(jones_band, stations[0], axis=1).reshape(
        direction_count, 2, 2, 2, baseline_count
    )
    station_second = jnp.take(jones_band, stations[1], axis=1).reshape(
        direction_count, 2, 2, 2, baseline_count
    )
    sky_model = coherent_band.astype(jnp.float32).reshape(direction_count, 2, 2, 2, baseline_count)
    inner_real, inner_imag = matrix_product(
        station_first[:, 0], station_first[:, 1], sky_model[:, 0], sky_model[:, 1]
    )
    herm_real = jnp.swapaxes(station_second[:, 0], 1, 2)
    herm_imag = -jnp.swapaxes(station_second[:, 1], 1, 2)
    model_real, model_imag = matrix_product(inner_real, inner_imag, herm_real, herm_imag)
    predicted = jnp.stack([jnp.sum(model_real, axis=0), jnp.sum(model_imag, axis=0)])
    misfit = visible_band.astype(jnp.float32).reshape(2, 2, 2, baseline_count) - predicted
    data_scale = jones_band.shape[1] / (2.0 * baseline_count)
    distance = jones_band - target_band
    return (
        data_scale * jnp.sum(misfit * misfit)
        + jnp.sum(multiplier_band * distance)
        + 0.5 * PENALTY * jnp.sum(weight_band[None, :] * distance * distance)
    )


def descend(
    jones_band, visible_band, coherent_band, stations, target_band, multiplier_band, weight_band
):
    slope_fn = jax.grad(band_loss)
    slope = slope_fn(
        jones_band, visible_band, coherent_band, stations, target_band, multiplier_band, weight_band
    )
    jones_band = jones_band - STEP_SIZE * slope
    return jones_band


def solve_normal(normal_matrix, right_side):
    gram_aa, gram_ab, gram_ac, gram_bb, gram_bc, gram_cc = [
        normal_matrix[position] for position in range(6)
    ]
    cofac_aa = gram_bb * gram_cc - gram_bc * gram_bc
    cofac_ab = gram_ac * gram_bc - gram_ab * gram_cc
    cofac_ac = gram_ab * gram_bc - gram_ac * gram_bb
    cofac_bb = gram_aa * gram_cc - gram_ac * gram_ac
    cofac_bc = gram_ab * gram_ac - gram_aa * gram_bc
    cofac_cc = gram_aa * gram_bb - gram_ab * gram_ab
    determinant = gram_aa * cofac_aa + gram_ab * cofac_ab + gram_ac * cofac_ac
    inverse_det = 1.0 / determinant
    first_term = right_side[0]
    second_term = right_side[1]
    third_term = right_side[2]
    coeff_a = (cofac_aa * first_term + cofac_ab * second_term + cofac_ac * third_term) * inverse_det
    coeff_b = (cofac_ab * first_term + cofac_bb * second_term + cofac_bc * third_term) * inverse_det
    coeff_c = (cofac_ac * first_term + cofac_bc * second_term + cofac_cc * third_term) * inverse_det
    return jnp.stack([coeff_a, coeff_b, coeff_c])


def local(jones_start, visible, coherent, stations, weights, multiplier_start):
    band_count = lax.axis_size("band")
    band_index = lax.axis_index("band")
    abscissa = -1.0 + 2.0 * band_index.astype(jnp.float32) / (band_count - 1)
    basis_local = (jnp.ones((), jnp.float32), abscissa, 1.5 * abscissa * abscissa - 0.5)
    weight_band = weights[0]
    visible_band = visible[0]
    coherent_band = coherent[0]
    station_share = weights.shape[1] // band_count
    products = jnp.stack(
        [basis_local[first_idx] * basis_local[second_idx] for first_idx, second_idx in PAIR_LIST]
    )
    normal_term = PENALTY * products[:, None] * weight_band[None, :]
    normal_solver = lax.psum(normal_term, "band")

    def iteration(turn_index, carried):
        jones_band, multiplier_band, owned_prior = carried
        combined = multiplier_band + PENALTY * weight_band[None, :] * jones_band
        weighted_terms = jnp.stack([basis_local[term_index] * combined for term_index in range(3)])
        full_sums = lax.psum(weighted_terms, "band")
        coefficients = solve_normal(normal_solver, full_sums)
        owned_coeff = lax.dynamic_slice_in_dim(
            coefficients, band_index * station_share, station_share, 2
        )
        target_band = (
            basis_local[0] * coefficients[0]
            + basis_local[1] * coefficients[1]
            + basis_local[2] * coefficients[2]
        )
        multiplier_band = multiplier_band + PENALTY * weight_band[None, :] * (
            jones_band - target_band
        )
        jones_band = descend(
            jones_band,
            visible_band,
            coherent_band,
            stations,
            target_band,
            multiplier_band,
            weight_band,
        )
        return (jones_band, multiplier_band, owned_coeff)

    owned_start = jnp.zeros((3, jones_start.shape[1], station_share), jnp.float32)
    jones_band, multiplier_band, owned_coeff = lax.fori_loop(
        0, ITERS, iteration, (jones_start[0], multiplier_start[0], owned_start)
    )
    coeff_rows = owned_coeff.reshape(
        owned_coeff.shape[0] * owned_coeff.shape[1], owned_coeff.shape[2]
    )
    return (jones_band[None], multiplier_band[None], coeff_rows)


def solution(mesh):
    return jax.shard_map(
        local,
        mesh=mesh,
        in_specs=(
            P("band", None, None),
            P("band", None, None),
            P("band", None, None),
            P(),
            P("band", None),
            P("band", None, None),
        ),
        out_specs=(P("band", None, None), P("band", None, None), P(None, "band")),
        check_vma=False,
    )
```

profile of v0, /device:TPU:0, one launch (start us, length us, event | category | flops | bytes accessed | tf_op | source)
XLA Modules:
  0.0 372.7 jit_solution(7236217893154198396)
XLA Ops:
  9.7 42.0 %psum.17 = f32[6,512]{1,0:T(8,128)S(1)} all-reduce(f32[6,512]{1,0:T(8,128)S(1)} %broadcast_multiply_fusion.1), channel_id=1, replica_groups=mesh['band'=32] {'band'}, use_global_device_ids=true, to_apply=%region_0.0 | all-reduce | flops 3072 | bytes 24576 | tf_op jit(solution)/shard_map/psum | solution.py:98
  52.3 312.1 %while.17 = (s32[]{:T(128)}, f32[32,512]{1,0:T(8,128)S(1)}, f32[32,512]{1,0:T(8,128)S(1)}, f32[3,32,16]{2,1,0:T(8,128)}, f32[1,512]{1,0:T(1,128)}, /*index=5*/f3...) while((s32[]{:T(128)}, f32[32,512]{1,0:T(8,128)S(1)}, ...), condition=%wide.region_27.0_spmd, body=%wide.region_1.28_spmd.sunk | while | flops 6967298 | bytes 52347996 | solution.py:129
  55.4 14.1 %gather_fusion.1 = f32[4096,32]{1,0:T(8,128)} fusion(f32[32,512]{0,1:T(8,128)S(1)} %copy.101, s32[4096]{0:T(1024)S(1)} %get-tuple-element.581), kind=kCustom, calls=%fused_computation.1.clone.clone.1 | custom fusion | bytes 1064960 | tf_op jit(solution)/shard_map/while/body/eval_jaxpr/jvp(jit(_take))/gather | solution.py:29
  69.5 3.6 select_bitcast_fusion.5
  74.0 0.9 copy.106
  76.6 14.1 %gather_fusion = f32[4096,32]{1,0:T(8,128)} fusion(f32[32,512]{0,1:T(8,128)S(1)} %copy.101, s32[4096]{0:T(1024)S(1)} %get-tuple-element.578), kind=kCustom, calls=%fused_computation.clone.clone.1 | custom fusion | bytes 1064960 | tf_op jit(solution)/shard_map/while/body/eval_jaxpr/jvp(jit(_take))/gather | solution.py:32
  90.6 3.6 select_bitcast_fusion.4
  98.0 1.3 multiply_reduce_fusion.26
  101.6 2.0 copy.114
  105.0 22.7 %scatter_custom_fusion.8 = f32[32,512]{0,1:T(8,128)S(1)} fusion(s32[4096]{0:T(1024)} %get-tuple-element.603, f32[4096,32]{1,0:T(8,128)} %copy.114, f32[]{:T(128)} %constant.70.clone.25..sunk), kind=kCustom, calls=%fused_computation.50.clone.1 | custom fusion | flops 131072 | bytes 66048 | tf_op jit(solution)/shard_map/while/body/eval_jaxpr/transpose(jvp(jit(_take)))/scatter-add | solution.py:29
  127.7 55.5 %all-reduce.6.cloned.1.call-done = f32[3,32,512]{2,1,0:T(8,128)} async-done(((f32[3,32,512]{2,1,0:T(8,128)}), f32[3,32,512]{2,1,0:T(8,128)}) %all-reduce.6.cloned.1.call-update) | async-done | bytes 196624 | tf_op jit(solution)/shard_map/while/body/eval_jaxpr/psum | solution.py:104
  183.2 1.0 add_add_fusion.2
  184.4 22.5 %scatter_fusion = f32[32,512]{0,1:T(8,128)S(1)} fusion(f32[32,512]{0,1:T(8,128)S(1)} %copy.102, s32[4096]{0:T(1024)S(1)} %get-tuple-element.577, f32[4096,32]{1,0:T(8,128)S(1)} %copy.112), kind=kCustom, calls=%fused_computation.2.clone.1 | custom fusion | flops 131072 | bytes 1589248 | tf_op jit(solution)/shard_map/while/body/eval_jaxpr/transpose(jvp(jit(_take)))/scatter-add | solution.py:32
  210.9 14.1 %gather_fusion.1 = f32[4096,32]{1,0:T(8,128)} fusion(f32[32,512]{0,1:T(8,128)S(1)} %copy.101, s32[4096]{0:T(1024)S(1)} %get-tuple-element.581), kind=kCustom, calls=%fused_computation.1.clone.clone.1 | custom fusion | bytes 1064960 | tf_op jit(solution)/shard_map/while/body/eval_jaxpr/jvp(jit(_take))/gather | solution.py:29
  225.0 3.6 select_bitcast_fusion.5
  232.0 14.1 %gather_fusion = f32[4096,32]{1,0:T(8,128)} fusion(f32[32,512]{0,1:T(8,128)S(1)} %copy.101, s32[4096]{0:T(1024)S(1)} %get-tuple-element.578), kind=kCustom, calls=%fused_computation.clone.clone.1 | custom fusion | bytes 1064960 | tf_op jit(solution)/shard_map/while/body/eval_jaxpr/jvp(jit(_take))/gather | solution.py:32
  246.1 3.6 select_bitcast_fusion.4
  253.5 1.3 multiply_reduce_fusion.26
  257.1 2.0 copy.114
  260.5 22.7 %scatter_custom_fusion.8 = f32[32,512]{0,1:T(8,128)S(1)} fusion(s32[4096]{0:T(1024)} %get-tuple-element.603, f32[4096,32]{1,0:T(8,128)} %copy.114, f32[]{:T(128)} %constant.70.clone.25..sunk), kind=kCustom, calls=%fused_computation.50.clone.1 | custom fusion | flops 131072 | bytes 66048 | tf_op jit(solution)/shard_map/while/body/eval_jaxpr/transpose(jvp(jit(_take)))/scatter-add | solution.py:29
  283.2 56.6 %all-reduce.6.cloned.1.call-done = f32[3,32,512]{2,1,0:T(8,128)} async-done(((f32[3,32,512]{2,1,0:T(8,128)}), f32[3,32,512]{2,1,0:T(8,128)}) %all-reduce.6.cloned.1.call-update) | async-done | bytes 196624 | tf_op jit(solution)/shard_map/while/body/eval_jaxpr/psum | solution.py:104
  339.8 1.0 add_add_fusion.2
  341.0 22.5 %scatter_fusion = f32[32,512]{0,1:T(8,128)S(1)} fusion(f32[32,512]{0,1:T(8,128)S(1)} %copy.102, s32[4096]{0:T(1024)S(1)} %get-tuple-element.577, f32[4096,32]{1,0:T(8,128)S(1)} %copy.112), kind=kCustom, calls=%fused_computation.2.clone.1 | custom fusion | flops 131072 | bytes 1589248 | tf_op jit(solution)/shard_map/while/body/eval_jaxpr/transpose(jvp(jit(_take)))/scatter-add | solution.py:32
  364.4 1.5 copy.85
  (171 shorter events, 31.7 us)
Async XLA Ops:
  52.3 130.9 %all-reduce.6.cloned.1.call-start = ((), (), s32[]{:S(2)}) async-start(), calls=%async_computation | async-start | bytes 393216 | tf_op jit(solution)/shard_map/while/body/eval_jaxpr/psum | solution.py:104
  73.7 2.1 copy-start.5
  94.8 1.1 copy-start.1
  96.7 1.3 copy-start.7
  104.0 79.2 %copy-start.8 = (f32[1,512]{1,0:T(1,128)S(1)}, f32[1,512]{1,0:T(1,128)}, u32[]{:S(2)}) copy-start(f32[1,512]{1,0:T(1,128)} %get-tuple-element.667) | copy-start | bytes 6148 | tf_op jit(solution)/shard_map/while
  104.0 79.2 %copy-start.9 = (f32[1,512]{1,0:T(1,128)S(1)}, f32[1,512]{1,0:T(1,128)}, u32[]{:S(2)}) copy-start(f32[1,512]{1,0:T(1,128)} %get-tuple-element.666) | copy-start | bytes 6148 | tf_op jit(solution)/shard_map/while
  104.0 79.2 %copy-start.10 = (f32[1,512]{1,0:T(1,128)S(1)}, f32[1,512]{1,0:T(1,128)}, u32[]{:S(2)}) copy-start(f32[1,512]{1,0:T(1,128)} %get-tuple-element.663) | copy-start | bytes 6148 | tf_op jit(solution)/shard_map/while
  104.0 79.2 %copy-start.11 = (f32[1,512]{1,0:T(1,128)S(1)}, f32[1,512]{1,0:T(1,128)}, u32[]{:S(2)}) copy-start(f32[1,512]{1,0:T(1,128)} %get-tuple-element.671) | copy-start | bytes 6148 | tf_op jit(solution)/shard_map/while
  104.0 79.2 %copy-start.12 = (f32[1,512]{1,0:T(1,128)S(1)}, f32[1,512]{1,0:T(1,128)}, u32[]{:S(2)}) copy-start(f32[1,512]{1,0:T(1,128)} %get-tuple-element.670) | copy-start | bytes 6148 | tf_op jit(solution)/shard_map/while
  104.0 79.2 %copy-start.13 = (f32[1,512]{1,0:T(1,128)S(1)}, f32[1,512]{1,0:T(1,128)}, u32[]{:S(2)}) copy-start(f32[1,512]{1,0:T(1,128)} %get-tuple-element.669) | copy-start | bytes 6148 | tf_op jit(solution)/shard_map/while
  184.4 22.7 %copy-start.2 = (f32[3,32,512]{2,1,0:T(8,128)S(1)}, f32[3,32,512]{2,1,0:T(8,128)}, u32[]{:S(2)}) copy-start(f32[3,32,512]{2,1,0:T(8,128)} %all-reduce.6.cloned.1.call-done) | copy-start | bytes 589828 | tf_op jit(solution)/shard_map/while
  207.8 132.0 %all-reduce.6.cloned.1.call-start = ((), (), s32[]{:S(2)}) async-start(), calls=%async_computation | async-start | bytes 393216 | tf_op jit(solution)/shard_map/while/body/eval_jaxpr/psum | solution.py:104
  229.1 2.1 copy-start.5
  250.3 1.1 copy-start.1
  252.2 1.3 copy-start.7
  259.5 80.3 %copy-start.8 = (f32[1,512]{1,0:T(1,128)S(1)}, f32[1,512]{1,0:T(1,128)}, u32[]{:S(2)}) copy-start(f32[1,512]{1,0:T(1,128)} %get-tuple-element.667) | copy-start | bytes 6148 | tf_op jit(solution)/shard_map/while
  259.5 80.3 %copy-start.9 = (f32[1,512]{1,0:T(1,128)S(1)}, f32[1,512]{1,0:T(1,128)}, u32[]{:S(2)}) copy-start(f32[1,512]{1,0:T(1,128)} %get-tuple-element.666) | copy-start | bytes 6148 | tf_op jit(solution)/shard_map/while
  259.5 80.3 %copy-start.10 = (f32[1,512]{1,0:T(1,128)S(1)}, f32[1,512]{1,0:T(1,128)}, u32[]{:S(2)}) copy-start(f32[1,512]{1,0:T(1,128)} %get-tuple-element.663) | copy-start | bytes 6148 | tf_op jit(solution)/shard_map/while
  259.5 80.3 %copy-start.11 = (f32[1,512]{1,0:T(1,128)S(1)}, f32[1,512]{1,0:T(1,128)}, u32[]{:S(2)}) copy-start(f32[1,512]{1,0:T(1,128)} %get-tuple-element.671) | copy-start | bytes 6148 | tf_op jit(solution)/shard_map/while
  259.5 80.3 %copy-start.12 = (f32[1,512]{1,0:T(1,128)S(1)}, f32[1,512]{1,0:T(1,128)}, u32[]{:S(2)}) copy-start(f32[1,512]{1,0:T(1,128)} %get-tuple-element.670) | copy-start | bytes 6148 | tf_op jit(solution)/shard_map/while
  259.5 80.3 %copy-start.13 = (f32[1,512]{1,0:T(1,128)S(1)}, f32[1,512]{1,0:T(1,128)}, u32[]{:S(2)}) copy-start(f32[1,512]{1,0:T(1,128)} %get-tuple-element.669) | copy-start | bytes 6148 | tf_op jit(solution)/shard_map/while
  341.0 22.7 %copy-start.2 = (f32[3,32,512]{2,1,0:T(8,128)S(1)}, f32[3,32,512]{2,1,0:T(8,128)}, u32[]{:S(2)}) copy-start(f32[3,32,512]{2,1,0:T(8,128)} %all-reduce.6.cloned.1.call-done) | copy-start | bytes 589828 | tf_op jit(solution)/shard_map/while
  364.4 1.5 copy-start.3
  364.4 1.5 copy-start.4
  (6 other events, 5.1 us)
Sparse Core Ops, SparseCore 0:
  58.6 124.5 all-reduce.5
  214.1 125.6 all-reduce.5
where the time goes:
time: 374 us; the launch traced here: 373 us
  other arithmetic  123 us (33%)
  waiting for transfers between devices  112 us (30%)
  local copies, waits for them, and re-layouts  80.8 us (22%)
  blocking collectives  42 us (11%)
  between operations  14 us (4%)
    psum x2, waiting for transfers between devices, iteration(): full_sums = lax.psum(weighted_terms, 'band')  112 us
    scatter-add x2, other arithmetic, band_loss(): jnp.take(jones_band, stations[0], axis=1)  45.4 us
    scatter-add x2, other arithmetic, band_loss(): jnp.take(jones_band, stations[1], axis=1)  45 us
    psum x1, blocking collectives, local(): normal_solver = lax.psum(normal_term, 'band')  42 us
    gather x2, local copies, waits for them, and re-layouts, band_loss(): jnp.take(jones_band, stations[1], axis=1)  28.2 us
    gather x2, local copies, waits for them, and re-layouts, band_loss(): jnp.take(jones_band, stations[0], axis=1)  28.2 us
    select_n x4, other arithmetic, band_loss(): jnp.take(jones_band, stations[0], axis=1)  8.44 us
  transfers between devices with their start and end apart: 2, of which 2 were waited for; matrix products, arithmetic and copies ran while one was open for 39% of the time, Pallas kernels for 0%

commit v1 on v0

v1 whole, which is shorter than its diff:
```python
import functools

import jax
import jax.numpy as jnp
from jax import lax
from jax.experimental import pallas as pl
from jax.experimental.pallas import tpu as pltpu
from jax.sharding import PartitionSpec as P

PENALTY = 1.0
STEP_SIZE = 0.05
MESH = pl.DeviceIdType.MESH
LANES = 128
SUB = 8
GROUP = LANES * SUB


def tile(index):
    return pl.ds(pl.multiple_of(index * SUB, SUB), SUB)


def cmul(a, b):
    return (a[0] * b[0] - a[1] * b[1], a[0] * b[1] + a[1] * b[0])


def cmul_conj(a, b):
    return (a[0] * b[0] + a[1] * b[1], a[1] * b[0] - a[0] * b[1])


def cadd(a, b):
    return (a[0] + b[0], a[1] + b[1])


def basis(f, n):
    x = -1.0 + f.astype(jnp.float32) * (2.0 / (n - 1))
    return x, 1.5 * x * x - 0.5


def kernel(
    n, jones_ref, vis_ref, coh_ref, st_ref, w_ref, mult_ref,
    jout_ref, mout_ref, cout_ref,
    jcur, mcur, cohv, visv, stv, oht, jgat, pbuf, dbuf, xbuf, acc,
    send_a1, recv_a1, send_b1, recv_b1, send_a2, recv_a2, send_b2, recv_b2,
    inv, coefs, ctile, send_sem, recv_sem,
):
    me = lax.axis_index("band")
    rows, stations = jones_ref.shape[1:]
    baselines = vis_ref.shape[2]
    chunks = stations // LANES
    groups = baselines // GROUP
    dirs = rows // 8
    share = stations // n
    scale = stations / (2.0 * baselines)
    all_own = n == rows
    is_owner = me < rows

    def when_owner(fn, otherwise=None):
        if all_own:
            fn()
        else:
            pl.when(is_owner)(fn)
            if otherwise is not None:
                pl.when(jnp.logical_not(is_owner))(otherwise)

    barrier = pltpu.get_barrier_semaphore()

    def greet_all():
        def body(i, _):
            pl.semaphore_signal(barrier, inc=1, device_id=(lax.rem(me + i, n),), device_id_type=MESH)
            return 0
        lax.fori_loop(1, n, body, 0)

    def greet_owners():
        def body(i, _):
            pl.semaphore_signal(barrier, inc=1, device_id=(i,), device_id_type=MESH)
            return 0
        lax.fori_loop(0, rows, body, 0)

    when_owner(greet_all, greet_owners)

    weight = w_ref[...]

    def fill_a(buf, m, j):
        comb = m + PENALTY * weight * j
        for h in range(chunks):
            cut = slice(h * LANES, (h + 1) * LANES)
            buf[pl.ds(h, rows, stride=SUB), :] = comb[:, cut]
            buf[pl.ds(chunks + h, rows, stride=SUB), :] = jnp.broadcast_to(weight[:, cut], (rows, LANES))

    def copy(src, s_idx, dst, d_idx, phase, dest):
        return pltpu.make_async_remote_copy(
            src_ref=src.at[tile(s_idx)], dst_ref=dst.at[tile(d_idx)],
            send_sem=send_sem.at[phase], recv_sem=recv_sem.at[phase],
            device_id=(dest,), device_id_type=MESH)

    def send_a(src, dst, phase):
        def body(i, _):
            c = lax.rem(me + i, rows)

            @pl.when(c != me)
            def _():
                copy(src, c, dst, me, phase, c).start()
            return 0

        if all_own:
            def body(i, _):
                c = lax.rem(me + i, rows)
                copy(src, c, dst, me, phase, c).start()
                return 0
            lax.fori_loop(1, rows, body, 0)
        else:
            lax.fori_loop(0, rows, body, 0)

        def own():
            dst[tile(me), :] = src[tile(me), :]
        when_owner(own)

    def send_b(src, dst, phase):
        def body(i, _):
            d = lax.rem(me + i, n)
            copy(src, d, dst, me, phase, d).start()
            return 0
        lax.fori_loop(1, n, body, 0)
        dst[tile(me), :] = src[tile(me), :]

    def wait_for(ref, slots, sem):
        part = ref.at[pl.ds(0, slots * SUB)]
        pltpu.make_async_copy(part, part, sem).wait()

    fill_a(send_a1, mult_ref[0], jones_ref[0])
    if all_own:
        pl.semaphore_wait(barrier, n - 1)
    else:
        when_owner(lambda: pl.semaphore_wait(barrier, n - 1), lambda: pl.semaphore_wait(barrier, rows))
    send_a(send_a1, recv_a1, 0)
    jcur[...] = jones_ref[0]

    def prep(g, _):
        for s in range(SUB):
            cut = pl.ds(pl.multiple_of(g * GROUP + s * LANES, LANES), LANES)
            cohv[g, pl.ds(s, rows, stride=SUB), :] = coh_ref[0, :, cut].astype(jnp.float32)
            visv[g, pl.ds(s, 8, stride=SUB), :] = vis_ref[0, :, cut].astype(jnp.float32)
            for side in range(2):
                ids = st_ref[side : side + 1, cut]
                stv[g, side * SUB + s : side * SUB + s + 1, :] = ids
                low = jnp.broadcast_to(ids & (LANES - 1), (LANES, LANES))
                hot = low == lax.broadcasted_iota(jnp.int32, (LANES, LANES), 0)
                oht[g, :, side * GROUP + s * LANES : side * GROUP + (s + 1) * LANES] = jnp.where(hot, 1.0, 0.0).astype(jnp.bfloat16)
        return 0

    lax.fori_loop(0, groups, prep, 0)

    def group_step(g, _):
        ids = [stv[g, side * SUB : (side + 1) * SUB, :] for side in range(2)]
        low = [v & (LANES - 1) for v in ids]
        high = [v >> 7 for v in ids]
        pick = [[v == h for h in range(1, chunks)] for v in high]

        def station_value(side, c):
            out = None
            for h in range(chunks):
                row = jnp.broadcast_to(jcur[c : c + 1, h * LANES : (h + 1) * LANES], (SUB, LANES))
                got = jnp.take_along_axis(row, low[side], axis=1)
                out = got if h == 0 else jnp.where(pick[side][h - 1], got, out)
            return out

        def comp(ref, k, i, j):
            base = k * 8 + i * 2 + j
            return (ref(base), ref(base + 4))

        def tiles(ref, offset):
            return lambda c: ref[(offset + c) * SUB : (offset + c + 1) * SUB, :]

        coh = lambda c: cohv[g, c * SUB : (c + 1) * SUB, :]
        vis = lambda c: visv[g, c * SUB : (c + 1) * SUB, :]
        model = [[None, None], [None, None]]
        for k in range(dirs):
            for c in range(k * 8, k * 8 + 8):
                jgat[c * SUB : (c + 1) * SUB, :] = station_value(0, c)
                jgat[(rows + c) * SUB : (rows + c + 1) * SUB, :] = station_value(1, c)
            a = [[comp(tiles(jgat, 0), k, i, j) for j in range(2)] for i in range(2)]
            q = [[comp(tiles(jgat, rows), k, i, j) for j in range(2)] for i in range(2)]
            m = [[comp(coh, k, i, j) for j in range(2)] for i in range(2)]
            for i in range(2):
                inner = [cadd(cmul(a[i][0], m[0][j]), cmul(a[i][1], m[1][j])) for j in range(2)]
                for j in range(2):
                    base = k * 8 + i * 2 + j
                    pbuf[base * SUB : (base + 1) * SUB, :] = inner[j][0]
                    pbuf[(base + 4) * SUB : (base + 5) * SUB, :] = inner[j][1]
                    term = cadd(cmul_conj(inner[0], q[j][0]), cmul_conj(inner[1], q[j][1]))
                    model[i][j] = term if model[i][j] is None else cadd(model[i][j], term)
        resid = [[None, None], [None, None]]
        for i in range(2):
            for j in range(2):
                v = comp(vis, 0, i, j)
                resid[i][j] = tuple((-2.0 * scale) * (v[z] - model[i][j][z]) for z in range(2))
        for k in range(dirs):
            q = [[comp(tiles(jgat, rows), k, i, j) for j in range(2)] for i in range(2)]
            m = [[comp(coh, k, i, j) for j in range(2)] for i in range(2)]
            p = [[comp(tiles(pbuf, 0), k, i, j) for j in range(2)] for i in range(2)]
            for i in range(2):
                x = [cadd(cmul(resid[i][0], q[0][l]), cmul(resid[i][1], q[1][l])) for l in range(2)]
                for j in range(2):
                    ga = cadd(cmul_conj(x[0], m[j][0]), cmul_conj(x[1], m[j][1]))
                    gq = cadd(cmul_conj(p[0][j], resid[0][i]), cmul_conj(p[1][j], resid[1][i]))
                    base = k * 8 + i * 2 + j
                    for z in range(2):
                        c = base + 4 * z
                        dbuf[c * SUB : (c + 1) * SUB, :] = ga[z]
                        dbuf[(rows + c) * SUB : (rows + c + 1) * SUB, :] = gq[z]
        for side in range(2):
            for s in range(SUB):
                d = dbuf[pl.ds(side * rows * SUB + s, rows, stride=SUB), :]
                big = d.astype(jnp.bfloat16)
                small = (d - big.astype(jnp.float32)).astype(jnp.bfloat16)
                which = jnp.broadcast_to(high[side][s : s + 1, :], (rows, LANES))
                at = slice(side * GROUP + s * LANES, side * GROUP + (s + 1) * LANES)
                for h in range(chunks):
                    mask = jnp.where(which == h, 1.0, 0.0).astype(jnp.bfloat16)
                    xbuf[(2 * h) * rows : (2 * h + 1) * rows, at] = big * mask
                    xbuf[(2 * h + 1) * rows : (2 * h + 2) * rows, at] = small * mask
        acc[...] += lax.dot_general(
            xbuf[...], oht[g], (((1,), (1,)), ((), ())), preferred_element_type=jnp.float32)
        return 0

    def data_slope():
        parts = [
            acc[2 * h * rows : (2 * h + 1) * rows, :] + acc[(2 * h + 1) * rows : (2 * h + 2) * rows, :]
            for h in range(chunks)
        ]
        return jnp.concatenate(parts, axis=1)

    row_id = lax.broadcasted_iota(jnp.int32, (SUB, LANES), 0)

    def solve(recv, send, last):
        zero = jnp.zeros((SUB, LANES), jnp.float32)
        if not last:
            def add(f, sums):
                x, y = basis(f, n)
                t = recv[tile(f), :]
                tx, ty = t * x, t * y
                new = (t, tx, ty, tx * x, tx * y, ty * y)
                return tuple(o + v for o, v in zip(sums, new))

            sums = lax.fori_loop(0, n, add, (zero,) * 6, unroll=4)
            aa, ab, ac, bb, bc, cc = [PENALTY * pltpu.roll(v, chunks, 0) for v in sums]
            c_aa = bb * cc - bc * bc
            c_ab = ac * bc - ab * cc
            c_ac = ab * bc - ac * bb
            c_bb = aa * cc - ac * ac
            c_bc = ab * ac - aa * bc
            c_cc = aa * bb - ab * ab
            det = aa * c_aa + ab * c_ab + ac * c_ac
            cof = (c_aa, c_ab, c_ac, c_bb, c_bc, c_cc, 1.0 / det)
            for i, v in enumerate(cof):
                inv[i * SUB : (i + 1) * SUB, :] = v
            right = sums[:3]
        else:
            def add(f, sums):
                x, y = basis(f, n)
                t = recv[tile(f), :]
                return (sums[0] + t, sums[1] + t * x, sums[2] + t * y)

            right = lax.fori_loop(0, n, add, (zero,) * 3, unroll=4)
            cof = [inv[i * SUB : (i + 1) * SUB, :] for i in range(7)]
        c_aa, c_ab, c_ac, c_bb, c_bc, c_cc, inv_det = cof
        r0, r1, r2 = right
        k0 = (c_aa * r0 + c_ab * r1 + c_ac * r2) * inv_det
        k1 = (c_ab * r0 + c_bb * r1 + c_bc * r2) * inv_det
        k2 = (c_ac * r0 + c_bc * r1 + c_cc * r2) * inv_det
        if last:
            ctile[...] = jnp.zeros_like(ctile)
            for p, v in enumerate((k0, k1, k2)):
                coefs[p * SUB : (p + 1) * SUB, :] = v
            for h in range(chunks):
                for p in range(3):
                    ctile[h * SUB + 4 + p : h * SUB + 5 + p, :] = coefs[p * SUB + h : p * SUB + h + 1, :]

        def put(f, _):
            x, y = basis(f, n)
            t = k0 + x * k1 + y * k2
            if last:
                t = jnp.where(row_id < chunks, t, ctile[tile((f * share) // LANES), :])
            send[tile(f), :] = t
            return 0

        lax.fori_loop(0, n, put, 0, unroll=4)

    def owner_turn(recv_a, send_bb, recv_bb, phase, last):
        def go():
            wait_for(recv_a, n - 1, recv_sem.at[phase])
            solve(recv_a, send_bb, last)
            send_b(send_bb, recv_bb, phase + 1)
        when_owner(go)

    def wait_b(recv_bb, phase):
        if all_own:
            wait_for(recv_bb, rows - 1, recv_sem.at[phase])
        else:
            when_owner(lambda: wait_for(recv_bb, rows - 1, recv_sem.at[phase]),
                       lambda: wait_for(recv_bb, rows, recv_sem.at[phase]))

    def target_of(recv_bb):
        return jnp.concatenate([recv_bb[pl.ds(h, rows, stride=SUB), :] for h in range(chunks)], axis=1)

    half = groups // 2

    acc[...] = jnp.zeros_like(acc)
    lax.fori_loop(0, half, group_step, 0)
    owner_turn(recv_a1, send_b1, recv_b1, 0, False)
    lax.fori_loop(half, groups, group_step, 0)
    wait_b(recv_b1, 1)
    jones = jcur[...]
    pull = PENALTY * weight * (jones - target_of(recv_b1))
    mult = mult_ref[0] + pull
    jones = jones - STEP_SIZE * (data_slope() + mult + pull)
    mcur[...] = mult
    jcur[...] = jones
    fill_a(send_a2, mult, jones)
    send_a(send_a2, recv_a2, 2)

    acc[...] = jnp.zeros_like(acc)
    lax.fori_loop(0, half, group_step, 0)
    owner_turn(recv_a2, send_b2, recv_b2, 2, True)
    lax.fori_loop(half, groups, group_step, 0)
    wait_b(recv_b2, 3)
    jones = jcur[...]
    pull = PENALTY * weight * (jones - target_of(recv_b2))
    mult = mcur[...] + pull
    mout_ref[0] = mult
    jout_ref[0] = jones - STEP_SIZE * (data_slope() + mult + pull)
    shift = lax.rem(LANES - lax.rem(me * share, LANES), LANES)
    for p in range(3):
        part = pltpu.roll(recv_b2[pl.ds(4 + p, rows, stride=SUB), :], shift, 1)
        cout_ref[p * rows : (p + 1) * rows, :] = part[:, :share]

    for buf, phase in ((send_a1, 0), (send_a2, 2)):
        if all_own:
            wait_for(buf, rows - 1, send_sem.at[phase])
        else:
            when_owner(functools.partial(wait_for, buf, rows - 1, send_sem.at[phase]),
                       functools.partial(wait_for, buf, rows, send_sem.at[phase]))
    for buf, phase in ((send_b1, 1), (send_b2, 3)):
        when_owner(functools.partial(wait_for, buf, n - 1, send_sem.at[phase]))


def solution(mesh):
    n = mesh.shape["band"]

    def local(jones, visible, coherent, stations, weights, mult):
        rows, count = jones.shape[1:]
        base = visible.shape[2]
        chunks = count // LANES
        groups = base // GROUP
        assert n >= rows and chunks == 4 and LANES % (count // n) == 0
        f32, bf16 = jnp.float32, jnp.bfloat16
        vm = pltpu.VMEM
        flat = lambda slots: vm((slots * SUB, LANES), f32)
        return pl.pallas_call(
            functools.partial(kernel, n),
            out_shape=(
                jax.ShapeDtypeStruct(jones.shape, f32),
                jax.ShapeDtypeStruct(jones.shape, f32),
                jax.ShapeDtypeStruct((3 * rows, count // n), f32),
            ),
            in_specs=[pl.BlockSpec(memory_space=vm)] * 6,
            out_specs=[pl.BlockSpec(memory_space=vm)] * 3,
            scratch_shapes=[
                vm((rows, count), f32),
                vm((rows, count), f32),
                vm((groups, rows * SUB, LANES), f32),
                vm((groups, 8 * SUB, LANES), f32),
                vm((groups, 2 * SUB, LANES), jnp.int32),
                vm((groups, LANES, 2 * GROUP), bf16),
                flat(2 * rows),
                flat(rows),
                flat(2 * rows),
                vm((2 * chunks * rows, 2 * GROUP), bf16),
                vm((2 * chunks * rows, LANES), f32),
                flat(rows), flat(n), flat(n), flat(rows),
                flat(rows), flat(n), flat(n), flat(rows),
                flat(7), flat(3), flat(chunks),
                pltpu.SemaphoreType.DMA((4,)),
                pltpu.SemaphoreType.DMA((4,)),
            ],
            compiler_params=pltpu.CompilerParams(
                collective_id=0, has_side_effects=True, vmem_limit_bytes=40 * 1024 * 1024),
        )(jones, visible, coherent, stations, weights, mult)

    return jax.shard_map(
        local,
        mesh=mesh,
        in_specs=(
            P("band", None, None), P("band", None, None), P("band", None, None),
            P(), P("band", None), P("band", None, None),
        ),
        out_specs=(P("band", None, None), P("band", None, None), P(None, "band")),
        check_vma=False,
    )
```

time: 374 us -> 36.9 us (0.10)
  other arithmetic: 123 us -> 0 us
  waiting for transfers between devices: 112 us -> 0 us
  local copies, waits for them, and re-layouts: 80.8 us -> 6.83 us
  blocking collectives: 42 us -> 0 us
  Pallas kernels: 0 us -> 29.1 us
  between operations: 14 us -> 0.65 us
    psum x2 -> x0, waiting for transfers between devices: 112 us -> none  [iteration(): full_sums = lax.psum(weighted_terms, 'band')]
    scatter-add x4 -> x0, other arithmetic: 90.4 us -> none  [the longest x2 45.4 us: band_loss(): jnp.take(jones_band, stations[0], axis=1)]
    gather x4 -> x0, local copies, waits for them, and re-layouts: 56.3 us -> none  [the longest x2 28.2 us: band_loss(): jnp.take(jones_band, stations[1], axis=1)]
    psum x1 -> x0, blocking collectives: 42 us -> none  [local(): normal_solver = lax.psum(normal_term, 'band')]
    pallas_call x0 -> x1, Pallas kernels: none -> 29.1 us  [local(): pl.pallas_call(functools.partial(kernel, n), out_shape=(jax.ShapeDtypeStr...]
    select_n x6 -> x0, other arithmetic: 15.7 us -> none  [the longest x4 8.44 us: band_loss(): jnp.take(jones_band, stations[0], axis=1)]
    reshape x13 -> x0, local copies, waits for them, and re-layouts: 9.29 us -> none  [the longest x6 5.27 us: band_loss(): jnp.take(jones_band, stations[0], axis=1)]
    reduce_sum x10 -> x0, other arithmetic: 7.3 us -> none  [the longest x4 3.84 us: contract(): lhs_part[:, :, :, None, :] * rhs_part[:, None, :, :, :]]
  transfers between devices with their start and end apart: 2 -> 0, of which waited for: 2 -> 0; matrix products, arithmetic and copies ran while one was open for 39% -> 0% of each run, Pallas kernels for 0% -> 0%
where the time goes in v1:
time: 36.9 us; the launch traced here: 36.5 us
  Pallas kernels  29.1 us (79%)
  local copies, waits for them, and re-layouts  6.83 us (19%)
  between operations  0.65 us (2%)
    pallas_call x1, Pallas kernels, local(): pl.pallas_call(functools.partial(kernel, n), out_shape=(jax.ShapeDtypeStr...  29.1 us
    unnamed x14, local copies, waits for them, and re-layouts  6.16 us

profile of v1, /device:TPU:0, one launch (start us, length us, event | category | flops | bytes accessed | tf_op | source)
XLA Modules:
  0.0 36.5 jit_solution(260006451926874621)
XLA Ops:
  0.6 0.0 copy-start
  0.6 0.9 %copy-done = bf16[1,32,4096]{2,1,0:T(8,128)(2,1)S(1)} copy-done((bf16[1,32,4096]{2,1,0:T(8,128)(2,1)S(1)}, bf16[1,32,4096]{2,1,0:T(8,128)(2,1)}, u32[]{:S(2)}) %copy-start) | copy-done | bytes 262168
  1.6 0.0 copy-start.1
  1.6 0.8 %copy-done.1 = f32[1,32,512]{2,1,0:T(8,128)S(1)} copy-done((f32[1,32,512]{2,1,0:T(8,128)S(1)}, f32[1,32,512]{2,1,0:T(8,128)}, u32[]{:S(2)}) %copy-start.1) | copy-done | bytes 65560
  2.4 0.0 copy-start.2
  2.4 0.8 %copy-done.2 = bf16[1,8,4096]{2,1,0:T(8,128)(2,1)S(1)} copy-done((bf16[1,8,4096]{2,1,0:T(8,128)(2,1)S(1)}, bf16[1,8,4096]{2,1,0:T(8,128)(2,1)}, u32[]{:S(2)}) %copy-start.2) | copy-done | bytes 65560
  3.3 0.0 copy-start.3
  3.3 0.8 %copy-done.3 = f32[1,32,512]{2,1,0:T(8,128)S(1)} copy-done((f32[1,32,512]{2,1,0:T(8,128)S(1)}, f32[1,32,512]{2,1,0:T(8,128)}, u32[]{:S(2)}) %copy-start.3) | copy-done | bytes 65560
  4.1 0.0 copy-start.4
  4.1 0.8 %copy-done.4 = s32[2,4096]{1,0:T(2,128)S(1)} copy-done((s32[2,4096]{1,0:T(2,128)S(1)}, s32[2,4096]{1,0:T(2,128)}, u32[]{:S(2)}) %copy-start.4) | copy-done | bytes 32792
  4.9 0.0 copy-start.5
  4.9 0.7 %copy-done.5 = f32[1,512]{1,0:T(1,128)S(1)} copy-done((f32[1,512]{1,0:T(1,128)S(1)}, f32[1,512]{1,0:T(1,128)}, u32[]{:S(2)}) %copy-start.5) | copy-done | bytes 2072
  5.5 29.1 %shard_map.85 = (f32[1,32,512]{2,1,0:T(8,128)S(1)}, f32[1,32,512]{2,1,0:T(8,128)S(1)}, f32[96,16]{1,0:T(8,128)S(1)}) custom-call(f32[1,32,512]{2,1,0:T(8,128)S(1)} %copy-done.1, bf16[1,8,4096]{2,1,0:T(8,128)(2,1)S(1)} %copy-done.2, bf16[1,32,4096]{2,1,0:T(8,128)(2,1)S(1)} %copy-done, s32[2,4096]{1,0:T(2,128)S(1)} %copy-done.4, f32[1,512]{1,0:T(1,128)S(1)} %copy-done.5, ...), custom_call_target="tpu_custom_call" | custom-call | tf_op jit(solution)/shard_map/pallas_call | solution.py:359
  34.6 0.7 %copy.9 = f32[96,16]{0,1:T(8,128)} copy(f32[96,16]{1,0:T(8,128)S(1)} %get-tuple-element.5) | data formatting | bytes 12288 | tf_op jit(solution)/shard_map/pallas_call | solution.py:359
  35.3 0.6 %copy.12 = f32[1,32,512]{2,1,0:T(8,128)} copy(f32[1,32,512]{2,1,0:T(8,128)S(1)} %get-tuple-element.9) | data formatting | bytes 131072
  35.9 0.6 %copy.13 = f32[1,32,512]{2,1,0:T(8,128)} copy(f32[1,32,512]{2,1,0:T(8,128)S(1)} %get-tuple-element.10) | data formatting | bytes 131072
Async XLA Ops:
  0.6 1.0 %copy-start = (bf16[1,32,4096]{2,1,0:T(8,128)(2,1)S(1)}, bf16[1,32,4096]{2,1,0:T(8,128)(2,1)}, u32[]{:S(2)}) copy-start(bf16[1,32,4096]{2,1,0:T(8,128)(2,1)} %coh_ref.1) | copy-start | bytes 786436
  1.6 0.8 %copy-start.1 = (f32[1,32,512]{2,1,0:T(8,128)S(1)}, f32[1,32,512]{2,1,0:T(8,128)}, u32[]{:S(2)}) copy-start(f32[1,32,512]{2,1,0:T(8,128)} %jones_ref.1) | copy-start | bytes 196612
  2.4 0.8 %copy-start.2 = (bf16[1,8,4096]{2,1,0:T(8,128)(2,1)S(1)}, bf16[1,8,4096]{2,1,0:T(8,128)(2,1)}, u32[]{:S(2)}) copy-start(bf16[1,8,4096]{2,1,0:T(8,128)(2,1)} %vis_ref.1) | copy-start | bytes 196612
  3.3 0.8 %copy-start.3 = (f32[1,32,512]{2,1,0:T(8,128)S(1)}, f32[1,32,512]{2,1,0:T(8,128)}, u32[]{:S(2)}) copy-start(f32[1,32,512]{2,1,0:T(8,128)} %mult_ref.1) | copy-start | bytes 196612
  4.1 0.8 %copy-start.4 = (s32[2,4096]{1,0:T(2,128)S(1)}, s32[2,4096]{1,0:T(2,128)}, u32[]{:S(2)}) copy-start(s32[2,4096]{1,0:T(2,128)} %st_ref.1) | copy-start | bytes 98308
  4.9 0.7 %copy-start.5 = (f32[1,512]{1,0:T(1,128)S(1)}, f32[1,512]{1,0:T(1,128)}, u32[]{:S(2)}) copy-start(f32[1,512]{1,0:T(1,128)} %w_ref.1) | copy-start | bytes 6148

commit v2 on v1

--- a/solution.py
+++ b/solution.py
@@ -37,12 +37,21 @@
 
 
 def kernel(
-    n, jones_ref, vis_ref, coh_ref, st_ref, w_ref, mult_ref,
+    n, jones_in, vis_in, coh_in, st_in, w_in, mult_in,
     jout_ref, mout_ref, cout_ref,
     jcur, mcur, cohv, visv, stv, oht, jgat, pbuf, dbuf, xbuf, acc,
     send_a1, recv_a1, send_b1, recv_b1, send_a2, recv_a2, send_b2, recv_b2,
     inv, coefs, ctile, send_sem, recv_sem,
+    jones_ref, vis_ref, coh_ref, st_ref, w_ref, mult_ref, load_sem,
 ):
+    loads = [
+        pltpu.make_async_copy(src, dst, load_sem.at[i])
+        for i, (src, dst) in enumerate((
+            (jones_in, jones_ref), (mult_in, mult_ref), (w_in, w_ref),
+            (coh_in, coh_ref), (vis_in, vis_ref), (st_in, st_ref)))
+    ]
+    for load in loads:
+        load.start()
     me = lax.axis_index("band")
     rows, stations = jones_ref.shape[1:]
     baselines = vis_ref.shape[2]
@@ -78,6 +87,8 @@
 
     when_owner(greet_all, greet_owners)
 
+    for load in loads[:3]:
+        load.wait()
     weight = w_ref[...]
 
     def fill_a(buf, m, j):
@@ -134,6 +145,8 @@
         when_owner(lambda: pl.semaphore_wait(barrier, n - 1), lambda: pl.semaphore_wait(barrier, rows))
     send_a(send_a1, recv_a1, 0)
     jcur[...] = jones_ref[0]
+    for load in loads[3:]:
+        load.wait()
 
     def prep(g, _):
         for s in range(SUB):
@@ -363,7 +376,7 @@
                 jax.ShapeDtypeStruct(jones.shape, f32),
                 jax.ShapeDtypeStruct((3 * rows, count // n), f32),
             ),
-            in_specs=[pl.BlockSpec(memory_space=vm)] * 6,
+            in_specs=[pl.BlockSpec(memory_space=pltpu.HBM)] * 6,
             out_specs=[pl.BlockSpec(memory_space=vm)] * 3,
             scratch_shapes=[
                 vm((rows, count), f32),
@@ -382,6 +395,8 @@
                 flat(7), flat(3), flat(chunks),
                 pltpu.SemaphoreType.DMA((4,)),
                 pltpu.SemaphoreType.DMA((4,)),
+                *[vm(v.shape, v.dtype) for v in (jones, visible, coherent, stations, weights, mult)],
+                pltpu.SemaphoreType.DMA((6,)),
             ],
             compiler_params=pltpu.CompilerParams(
                 collective_id=0, has_side_effects=True, vmem_limit_bytes=40 * 1024 * 1024),

time: 36.9 us -> 37.3 us (1.011)
  no operation moved by 1% of the time
where the time goes in v2:
time: 37.3 us; the launch traced here: 36.9 us
  Pallas kernels  29.4 us (79%)
  local copies, waits for them, and re-layouts  6.83 us (18%)
  between operations  0.65 us (2%)
    pallas_call x1, Pallas kernels, local(): pl.pallas_call(functools.partial(kernel, n), out_shape=(jax.ShapeDtypeStr...  29.4 us
    unnamed x14, local copies, waits for them, and re-layouts  6.16 us

profile of v2, /device:TPU:0, one launch (start us, length us, event | category | flops | bytes accessed | tf_op | source)
XLA Modules:
  0.0 36.9 jit_solution(838617527007856683)
XLA Ops:
  0.6 0.0 copy-start
  0.6 0.9 %copy-done = bf16[1,32,4096]{2,1,0:T(8,128)(2,1)S(1)} copy-done((bf16[1,32,4096]{2,1,0:T(8,128)(2,1)S(1)}, bf16[1,32,4096]{2,1,0:T(8,128)(2,1)}, u32[]{:S(2)}) %copy-start) | copy-done | bytes 262168
  1.6 0.0 copy-start.1
  1.6 0.8 %copy-done.1 = f32[1,32,512]{2,1,0:T(8,128)S(1)} copy-done((f32[1,32,512]{2,1,0:T(8,128)S(1)}, f32[1,32,512]{2,1,0:T(8,128)}, u32[]{:S(2)}) %copy-start.1) | copy-done | bytes 65560
  2.4 0.0 copy-start.2
  2.4 0.8 %copy-done.2 = bf16[1,8,4096]{2,1,0:T(8,128)(2,1)S(1)} copy-done((bf16[1,8,4096]{2,1,0:T(8,128)(2,1)S(1)}, bf16[1,8,4096]{2,1,0:T(8,128)(2,1)}, u32[]{:S(2)}) %copy-start.2) | copy-done | bytes 65560
  3.3 0.0 copy-start.3
  3.3 0.8 %copy-done.3 = f32[1,32,512]{2,1,0:T(8,128)S(1)} copy-done((f32[1,32,512]{2,1,0:T(8,128)S(1)}, f32[1,32,512]{2,1,0:T(8,128)}, u32[]{:S(2)}) %copy-start.3) | copy-done | bytes 65560
  4.1 0.0 copy-start.4
  4.1 0.8 %copy-done.4 = s32[2,4096]{1,0:T(2,128)S(1)} copy-done((s32[2,4096]{1,0:T(2,128)S(1)}, s32[2,4096]{1,0:T(2,128)}, u32[]{:S(2)}) %copy-start.4) | copy-done | bytes 32792
  4.9 0.0 copy-start.5
  4.9 0.7 %copy-done.5 = f32[1,512]{1,0:T(1,128)S(1)} copy-done((f32[1,512]{1,0:T(1,128)S(1)}, f32[1,512]{1,0:T(1,128)}, u32[]{:S(2)}) %copy-start.5) | copy-done | bytes 2072
  5.5 29.4 %shard_map.85 = (f32[1,32,512]{2,1,0:T(8,128)S(1)}, f32[1,32,512]{2,1,0:T(8,128)S(1)}, f32[96,16]{1,0:T(8,128)S(1)}) custom-call(f32[1,32,512]{2,1,0:T(8,128)S(1)} %copy-done.1, bf16[1,8,4096]{2,1,0:T(8,128)(2,1)S(1)} %copy-done.2, bf16[1,32,4096]{2,1,0:T(8,128)(2,1)S(1)} %copy-done, s32[2,4096]{1,0:T(2,128)S(1)} %copy-done.4, f32[1,512]{1,0:T(1,128)S(1)} %copy-done.5, ...), custom_call_target="tpu_custom_call" | custom-call | tf_op jit(solution)/shard_map/pallas_call | solution.py:372
  35.0 0.7 %copy.9 = f32[96,16]{0,1:T(8,128)} copy(f32[96,16]{1,0:T(8,128)S(1)} %get-tuple-element.5) | data formatting | bytes 12288 | tf_op jit(solution)/shard_map/pallas_call | solution.py:372
  35.6 0.6 %copy.12 = f32[1,32,512]{2,1,0:T(8,128)} copy(f32[1,32,512]{2,1,0:T(8,128)S(1)} %get-tuple-element.9) | data formatting | bytes 131072
  36.3 0.6 %copy.13 = f32[1,32,512]{2,1,0:T(8,128)} copy(f32[1,32,512]{2,1,0:T(8,128)S(1)} %get-tuple-element.10) | data formatting | bytes 131072
Async XLA Ops:
  0.6 1.0 %copy-start = (bf16[1,32,4096]{2,1,0:T(8,128)(2,1)S(1)}, bf16[1,32,4096]{2,1,0:T(8,128)(2,1)}, u32[]{:S(2)}) copy-start(bf16[1,32,4096]{2,1,0:T(8,128)(2,1)} %coh_in.1) | copy-start | bytes 786436
  1.6 0.8 %copy-start.1 = (f32[1,32,512]{2,1,0:T(8,128)S(1)}, f32[1,32,512]{2,1,0:T(8,128)}, u32[]{:S(2)}) copy-start(f32[1,32,512]{2,1,0:T(8,128)} %jones_in.1) | copy-start | bytes 196612
  2.4 0.8 %copy-start.2 = (bf16[1,8,4096]{2,1,0:T(8,128)(2,1)S(1)}, bf16[1,8,4096]{2,1,0:T(8,128)(2,1)}, u32[]{:S(2)}) copy-start(bf16[1,8,4096]{2,1,0:T(8,128)(2,1)} %vis_in.1) | copy-start | bytes 196612
  3.3 0.8 %copy-start.3 = (f32[1,32,512]{2,1,0:T(8,128)S(1)}, f32[1,32,512]{2,1,0:T(8,128)}, u32[]{:S(2)}) copy-start(f32[1,32,512]{2,1,0:T(8,128)} %mult_in.1) | copy-start | bytes 196612
  4.1 0.8 %copy-start.4 = (s32[2,4096]{1,0:T(2,128)S(1)}, s32[2,4096]{1,0:T(2,128)}, u32[]{:S(2)}) copy-start(s32[2,4096]{1,0:T(2,128)} %st_in.1) | copy-start | bytes 98308
  4.9 0.7 %copy-start.5 = (f32[1,512]{1,0:T(1,128)S(1)}, f32[1,512]{1,0:T(1,128)}, u32[]{:S(2)}) copy-start(f32[1,512]{1,0:T(1,128)} %w_in.1) | copy-start | bytes 6148

commit v3 on v2

--- a/solution.py
+++ b/solution.py
@@ -399,7 +399,7 @@
                 pltpu.SemaphoreType.DMA((6,)),
             ],
             compiler_params=pltpu.CompilerParams(
-                collective_id=0, has_side_effects=True, vmem_limit_bytes=40 * 1024 * 1024),
+                collective_id=0, has_side_effects=True, vmem_limit_bytes=64 * 1024 * 1024),
         )(jones, visible, coherent, stations, weights, mult)
 
     return jax.shard_map(

time: 37.3 us -> 34.3 us (0.920)
  local copies, waits for them, and re-layouts: 6.83 us -> 3.61 us
  Pallas kernels: 29.4 us -> 29.8 us
    unnamed x14 -> x4, local copies, waits for them, and re-layouts: 6.16 us -> 2.14 us
    pallas_call x1, local copies, waits for them, and re-layouts: 0.67 us -> 1.47 us  [local(): pl.pallas_call(functools.partial(kernel, n), out_shape=(jax.ShapeDtypeStr...]
    pallas_call x1, Pallas kernels: 29.4 us -> 29.8 us  [local(): pl.pallas_call(functools.partial(kernel, n), out_shape=(jax.ShapeDtypeStr...]
where the time goes in v3:
time: 34.3 us; the launch traced here: 34.1 us
  Pallas kernels  29.8 us (87%)
  local copies, waits for them, and re-layouts  3.61 us (11%)
  between operations  0.64 us (2%)
    pallas_call x1, Pallas kernels, local(): pl.pallas_call(functools.partial(kernel, n), out_shape=(jax.ShapeDtypeStr...  29.8 us
    unnamed x4, local copies, waits for them, and re-layouts  2.14 us
    pallas_call x1, local copies, waits for them, and re-layouts, local(): pl.pallas_call(functools.partial(kernel, n), out_shape=(jax.ShapeDtypeStr...  1.47 us

profile of v3, /device:TPU:0, one launch (start us, length us, event | category | flops | bytes accessed | tf_op | source)
XLA Modules:
  0.0 34.1 jit_solution(8513362810262993545)
XLA Ops:
  0.6 29.8 %shard_map.85 = (f32[1,32,512]{2,1,0:T(8,128)}, f32[1,32,512]{2,1,0:T(8,128)}, f32[96,16]{1,0:T(8,128)}) custom-call(f32[1,32,512]{2,1,0:T(8,128)} %jones_in.1, bf16[1,8,4096]{2,1,0:T(8,128)(2,1)} %vis_in.1, bf16[1,32,4096]{2,1,0:T(8,128)(2,1)} %coh_in.1, s32[2,4096]{1,0:T(2,128)} %st_in.1, f32[1,512]{1,0:T(1,128)} %w_in.1, f32[1,32,512]{2,1,0:T(8,128)} %mult_in.1), custom_call_target="tpu_custom_call" | custom-call | tf_op jit(solution)/shard_map/pallas_call | solution.py:372
  30.4 1.5 %copy.9 = f32[96,16]{0,1:T(8,128)} copy(f32[96,16]{1,0:T(8,128)} %get-tuple-element.5) | data formatting | bytes 12288 | tf_op jit(solution)/shard_map/pallas_call | solution.py:372
  31.9 0.0 copy-start
  31.9 1.5 %copy.12 = f32[1,32,512]{2,1,0:T(8,128)} copy(f32[1,32,512]{2,1,0:T(8,128)} %get-tuple-element.9) | data formatting | bytes 131072
  33.4 0.0 copy-done
  33.4 0.6 %copy.13 = f32[1,32,512]{2,1,0:T(8,128)} copy(f32[1,32,512]{2,1,0:T(8,128)S(1)} %copy-done) | data formatting | bytes 131072
Async XLA Ops:
  31.9 1.5 %copy-start = (f32[1,32,512]{2,1,0:T(8,128)S(1)}, f32[1,32,512]{2,1,0:T(8,128)}, u32[]{:S(2)}) copy-start(f32[1,32,512]{2,1,0:T(8,128)} %get-tuple-element.10) | copy-start | bytes 196612
